TPU v7x, 32 devices: a whole 2x2x4 slice. The times are simulated.
32 devices in a mesh: seq: 16 (over z, y, x), head: 2 (over core).
Axes of the slice: x: 2, y: 2, z: 4, core: 2. Of those that a mesh axis runs over, the one named last changes fastest.
Arguments:
- tokens: bfloat16 [16384, 2048], P('seq'), may hold values from -6 to 6
- w_query: bfloat16 [2048, 256], P(None, 'head'), may hold values from -0.25 to 0.25
- w_key: bfloat16 [2048, 256], P(None, 'head'), may hold values from -0.25 to 0.25
- w_value: bfloat16 [2048, 2048], P(None, 'head'), may hold values from -0.125 to 0.125
- w_out: bfloat16 [2048, 2048], replicated, may hold values from -1.796875 to 1.796875
Outputs:
- mixed: bfloat16 [16384, 2048], P('seq', 'head')
All inputs are finite; a program needn't handle non-finite values.
Results may differ from a plain program's by a relative error of at most 0.011.
Values may be sent and summed in bfloat16 or wider, within the bound.
A program may use at most 128 MiB of HBM per device.

v0:
```python
import functools

import jax
import jax.numpy as jnp
from jax import lax
from jax.experimental import pallas as pl
from jax.experimental.pallas import tpu as pltpu
from jax.sharding import PartitionSpec as P

KEY_DIM = 16
VALUE_DIM = 128
ROWS = 160
PAIR = 2
LOADS = 4
MESH = pl.DeviceIdType.MESH
F32 = jnp.float32
BF16 = jnp.bfloat16


def features(u, tail_one, square):
    n = u.shape[1]
    twice = jnp.concatenate([u, u], axis=0)
    parts = [u, u * u * square]
    for d in range(1, KEY_DIM // 2):
        parts.append(u * twice[d : d + KEY_DIM])
    half = KEY_DIM // 2
    parts.append(u[:half] * u[half:])
    row = lax.broadcasted_iota(jnp.int32, (8, n), 0)
    parts.append(jnp.where(row == 0, tail_one, 0.0))
    return jnp.concatenate(parts, axis=0)


def pack_norm(total):
    state, norm = total[:, :VALUE_DIM], total[:, VALUE_DIM:]
    top = norm[:VALUE_DIM]
    rest = norm[VALUE_DIM:]

    def diagonal(block):
        r = lax.broadcasted_iota(jnp.int32, block.shape, 0)
        l = lax.broadcasted_iota(jnp.int32, block.shape, 1)
        return jnp.sum(jnp.where(r == l, block, 0.0), axis=0, keepdims=True)

    first, second = diagonal(top), diagonal(rest)
    r = lax.broadcasted_iota(jnp.int32, (8, VALUE_DIM), 0)
    tail = jnp.where(r == 0, state[ROWS - 8 :], jnp.where(r == 1, first, jnp.where(r == 2, second, 0.0)))
    return jnp.concatenate([state[: ROWS - 8], tail], axis=0)


def unpack_norm(packed):
    tail = packed[ROWS - 8 :]

    def column(row, height):
        r = lax.broadcasted_iota(jnp.int32, (height, VALUE_DIM), 0)
        l = lax.broadcasted_iota(jnp.int32, (height, VALUE_DIM), 1)
        return jnp.sum(jnp.where(r == l, row, 0.0), axis=1, keepdims=True)

    return jnp.concatenate([column(tail[1:2], VALUE_DIM), column(tail[2:3], ROWS - VALUE_DIM)], axis=0)


def kernel(
    n_seq, chunk,
    tok_hbm, wq_hbm, wk_hbm, wv_hbm, wo_hbm, out_ref,
    tok, wqk, wv, wo, vals, qs, qt, kt, local, inner, qfeat, att,
    own, base, plane, send_x, recv_x, send_y, recv_y, send_z, recv_z,
    acc, load_sem, tok_sem, v_sem, x_ss, x_rs, y_ss, y_rs, z_ss, z_rs, a_ss, a_rs,
):
    rows, width = tok.shape
    heads = vals.shape[0]
    groups = heads // PAIR
    chunks = rows // chunk
    cols_here = wo.shape[1]
    chain = n_seq // 4
    seq = lax.axis_index("seq")
    core = lax.axis_index("head")
    x = lax.rem(seq, 2)
    y = lax.rem(seq // 2, 2)
    z = seq // 4
    x_peer = seq + 1 - 2 * x
    y_peer = seq + 2 - 4 * y
    up = lax.rem(seq + 4, n_seq)
    down = lax.rem(seq + n_seq - 4, n_seq)

    half = rows // LOADS
    load_w = [
        pltpu.make_async_copy(wk_hbm, wqk.at[:, pl.ds(128, 128)], load_sem.at[1]),
        pltpu.make_async_copy(wq_hbm, wqk.at[:, pl.ds(0, 128)], load_sem.at[0]),
    ]
    load_t = [
        pltpu.make_async_copy(tok_hbm.at[pl.ds(i * half, half)], tok.at[pl.ds(i * half, half)], tok_sem.at[i])
        for i in range(LOADS)
    ]
    load_o = pltpu.make_async_copy(
        wo_hbm.at[:, pl.ds(pl.multiple_of(core * cols_here, 128), cols_here)], wo, load_sem.at[2]
    )

    def load_v(g):
        at = pl.ds(pl.multiple_of(g * (PAIR * VALUE_DIM), 128), PAIR * VALUE_DIM)
        return pltpu.make_async_copy(wv_hbm.at[:, at], wv.at[:, at], v_sem.at[g])

    for c in load_w:
        c.start()
    for c in load_t:
        c.start()
    for g in range(groups):
        load_v(g).start()

    barrier = pltpu.get_barrier_semaphore()
    for peer in (x_peer, y_peer, up, down):
        pl.semaphore_signal(barrier, inc=1, device_id=(peer, core), device_id_type=MESH)
    pl.semaphore_signal(barrier, inc=1, device_id=(seq, 1 - core), device_id_type=MESH)

    def copy_x(g):
        return pltpu.make_async_remote_copy(
            src_ref=send_x.at[g], dst_ref=recv_x.at[g], send_sem=x_ss.at[g], recv_sem=x_rs.at[g],
            device_id=(x_peer, core), device_id_type=MESH)

    def copy_y(g):
        return pltpu.make_async_remote_copy(
            src_ref=send_y.at[g], dst_ref=recv_y.at[g], send_sem=y_ss.at[g], recv_sem=y_rs.at[g],
            device_id=(y_peer, core), device_id_type=MESH)

    def copy_z(g):
        return pltpu.make_async_remote_copy(
            src_ref=send_z.at[g], dst_ref=recv_z.at[g], send_sem=z_ss.at[g], recv_sem=z_rs.at[g],
            device_id=(up, core), device_id_type=MESH)

    def copy_a(g):
        at = pl.ds(pl.multiple_of(core * (heads * VALUE_DIM) + g * (PAIR * VALUE_DIM), 128), PAIR * VALUE_DIM)
        return pltpu.make_async_remote_copy(
            src_ref=att.at[:, at], dst_ref=att.at[:, at], send_sem=a_ss.at[g], recv_sem=a_rs.at[g],
            device_id=(seq, 1 - core), device_id_type=MESH)

    def pump(t):
        gx, gy, gz = t - 3, t - 6, t - 6 - 3 * z

        @pl.when((gx >= 0) & (gx < heads))
        def _():
            copy_x(gx).wait_recv()
            other = recv_x[gx].astype(F32)
            both = own[gx] + other
            send_y[gx] = both.astype(BF16)
            copy_y(gx).start()
            plane[gx] = both
            base[gx] = jnp.where(x == 1, other, 0.0)

        @pl.when((gy >= 0) & (gy < heads))
        def _():
            copy_y(gy).wait_recv()
            other = recv_y[gy].astype(F32)
            plane[gy] = plane[gy] + other
            base[gy] = base[gy] + jnp.where(y == 1, other, 0.0)

        @pl.when((gz >= 0) & (gz < heads) & (z < chain - 1))
        def _():
            @pl.when(z > 0)
            def _():
                copy_z(gz).wait_recv()
                earlier = recv_z[gz].astype(F32)
                base[gz] = base[gz] + earlier
                plane[gz] = plane[gz] + earlier

            send_z[gz] = plane[gz].astype(BF16)
            copy_z(gz).start()

    for c in load_w:
        c.wait()
    for i in range(LOADS):
        load_t[i].wait()
        part = pl.ds(i * half, half)
        qk = jnp.dot(tok[part], wqk[...], preferred_element_type=F32).astype(BF16).astype(F32)
        q = qk[:, :128] * 0.25
        qs[part] = q.astype(BF16)
        qt[:, part] = q.T
        kt[:, part] = qk[:, 128:].T
    load_o.start()
    pl.semaphore_wait(barrier, 5)

    def head_rows(h):
        return pl.ds(pl.multiple_of(h * KEY_DIM, KEY_DIM), KEY_DIM)

    def group_step(g, _):
        at = pl.ds(pl.multiple_of(g * (PAIR * VALUE_DIM), 128), PAIR * VALUE_DIM)
        load_v(g).wait()
        v = jnp.dot(tok[...], wv[:, at], preferred_element_type=F32).astype(BF16)
        for i in range(PAIR):
            vals[g * PAIR + i] = v[:, i * VALUE_DIM : (i + 1) * VALUE_DIM]
        ones = jnp.ones((chunk, VALUE_DIM), BF16)
        for i in range(PAIR):
            h = g * PAIR + i
            total = jnp.zeros((ROWS, 2 * VALUE_DIM), F32)
            for c in range(chunks):
                local[h, c] = total
                feat = features(kt[head_rows(h), pl.ds(c * chunk, chunk)], 1.0, 1.0).astype(BF16)
                wide = jnp.concatenate([vals[h, pl.ds(c * chunk, chunk)], ones], axis=1)
                total = total + jnp.dot(feat, wide, preferred_element_type=F32)
            packed = pack_norm(total)
            own[h] = packed
            send_x[h] = packed.astype(BF16)
            copy_x(h).start()
            pump(h)
        return 0

    lax.fori_loop(0, groups, group_step, 0)

    def inner_head(h):
        row_head = lax.broadcasted_iota(jnp.int32, (128, chunk), 0) // KEY_DIM
        r = lax.broadcasted_iota(jnp.int32, (chunk, chunk), 0)
        l = lax.broadcasted_iota(jnp.int32, (chunk, chunk), 1)
        ones = jnp.ones((chunk, VALUE_DIM), BF16)
        for c in range(chunks):
            span = pl.ds(c * chunk, chunk)
            k_own = jnp.where(row_head == h, kt[:, span], 0.0).astype(BF16)
            s = jnp.dot(qs[span], k_own, preferred_element_type=F32)
            s1 = s + 1.0
            taylor = jnp.where(l <= r, 0.5 * (s1 * s1) + 0.5, 0.0).astype(BF16)
            wide = jnp.concatenate([vals[h, span], ones], axis=1)
            inner[h, span] = jnp.dot(taylor, wide, preferred_element_type=F32)
            feat = features(qt[head_rows(h), span], 1.0, 0.5)
            qfeat[h, span] = feat.T.astype(BF16)

    def inner_step(g, _):
        for i in range(PAIR):
            inner_head(g * PAIR + i)
        pump(heads + g)
        return 0

    lax.fori_loop(0, groups, inner_step, 0)

    first = heads + groups

    def pumped(g):
        return jnp.maximum(first + 1 + g, PAIR * (g + 1) + 6 + 3 * (chain - 2))

    def rest(t, _):
        pump(t)
        return 0

    def outer_step(g):
        lax.fori_loop(jnp.where(g == 0, first, pumped(g - 1)), pumped(g), rest, 0)
        for i in range(PAIR):
            h = g * PAIR + i

            @pl.when(z == chain - 1)
            def _():
                copy_z(h).wait_recv()
                base[h] = base[h] + recv_z[h].astype(F32)

            packed = base[h]
            norm = jnp.broadcast_to(unpack_norm(packed), (ROWS, VALUE_DIM))
            entering = jnp.concatenate([packed, norm], axis=1)
            for c in range(chunks):
                span = pl.ds(c * chunk, chunk)
                prefix = (entering + local[h, c]).astype(BF16)
                total = inner[h, span] + jnp.dot(qfeat[h, span], prefix, preferred_element_type=F32)
                result = total[:, :VALUE_DIM] / total[:, VALUE_DIM:]
                at = pl.ds(pl.multiple_of(core * (heads * VALUE_DIM) + h * VALUE_DIM, 128), VALUE_DIM)
                att[span, at] = result.astype(BF16)
        copy_a(g).start()

    own_at, peer_at = core * (heads * VALUE_DIM), (1 - core) * (heads * VALUE_DIM)
    step = PAIR * VALUE_DIM

    def out_step(g, begin, end):
        here = pl.ds(pl.multiple_of(own_at + g * step, 128), step)
        there = pl.ds(pl.multiple_of(peer_at + g * step, 128), step)
        pltpu.make_async_remote_copy(
            src_ref=att.at[:, there], dst_ref=att.at[:, there], send_sem=a_ss.at[g], recv_sem=a_rs.at[g],
            device_id=(seq, 1 - core), device_id_type=MESH).wait_recv()

        def block(b, _):
            at = pl.ds(pl.multiple_of(b * 256, 128), 256)
            both = jnp.concatenate([att[:, here], att[:, there]], axis=1)
            part = jnp.dot(both, jnp.concatenate([wo[here, at], wo[there, at]], axis=0), preferred_element_type=F32)
            if not begin:
                part = part + acc[:, at]
            if end:
                out_ref[:, at] = part.astype(BF16)
            else:
                acc[:, at] = part
            return 0

        lax.fori_loop(0, cols_here // 256, block, 0)

    outer_step(0)
    load_o.wait()
    outer_step(1)
    out_step(0, True, False)

    def later(g, _):
        outer_step(g)
        out_step(g - 1, False, False)
        return 0

    lax.fori_loop(2, groups, later, 0)
    out_step(groups - 1, False, True)

    def finish(g, _):
        copy_a(g).wait_send()
        for i in range(PAIR):
            h = g * PAIR + i
            copy_x(h).wait_send()
            copy_y(h).wait_send()

            @pl.when(z < chain - 1)
            def _():
                copy_z(h).wait_send()

        return 0

    lax.fori_loop(0, groups, finish, 0)


def per_device(tokens, w_query, w_key, w_value, w_out):
    n_seq = lax.axis_size("seq")
    rows, width = tokens.shape
    heads = w_query.shape[1] // KEY_DIM
    groups = heads // PAIR
    chunk = min(256, rows)
    cols = w_out.shape[1] // lax.axis_size("head")
    vm = pltpu.VMEM
    slot = (heads, ROWS, VALUE_DIM)
    dma = pltpu.SemaphoreType.DMA
    return pl.pallas_call(
        functools.partial(kernel, n_seq, chunk),
        out_shape=jax.ShapeDtypeStruct((rows, cols), BF16),
        in_specs=[pl.BlockSpec(memory_space=pl.ANY)] * 5,
        out_specs=pl.BlockSpec(memory_space=pltpu.VMEM),
        scratch_shapes=[
            vm((rows, width), BF16),
            vm((width, 256), BF16),
            vm(w_value.shape, BF16),
            vm((w_out.shape[0], cols), BF16),
            vm((heads, rows, VALUE_DIM), BF16),
            vm((rows, 128), BF16),
            vm((128, rows), F32),
            vm((128, rows), F32),
            vm((heads, rows // chunk, ROWS, 2 * VALUE_DIM), F32),
            vm((heads, rows, 2 * VALUE_DIM), F32),
            vm((heads, rows, ROWS), BF16),
            vm((rows, w_out.shape[0]), BF16),
            vm(slot, F32), vm(slot, F32), vm(slot, F32),
            vm(slot, BF16), vm(slot, BF16), vm(slot, BF16), vm(slot, BF16), vm(slot, BF16), vm(slot, BF16),
            vm((rows, cols), F32),
            dma((3,)), dma((LOADS,)), dma((groups,)),
            dma((heads,)), dma((heads,)), dma((heads,)), dma((heads,)), dma((heads,)), dma((heads,)),
            dma((groups,)), dma((groups,)),
        ],
        compiler_params=pltpu.CompilerParams(
            collective_id=0, has_side_effects=True, vmem_limit_bytes=50 * 1024 * 1024
        ),
    )(tokens, w_query, w_key, w_value, w_out)


def solution(mesh):
    in_specs = (P("seq", None), P(None, "head"), P(None, "head"), P(None, "head"), P())
    return jax.shard_map(
        per_device, mesh=mesh, in_specs=in_specs, out_specs=P("seq", "head"), check_vma=False
    )
```

profile of v0, /device:TPU:25, one launch (start us, length us, event | category | flops | bytes accessed | tf_op | source)
XLA Modules:
  0.0 40.0 jit_solution(6743987877843633413)
XLA Ops:
  0.0 0.0 copy-start
  0.0 1.0 %copy-done = bf16[2048,128]{1,0:T(8,128)(2,1)S(1)} copy-done((bf16[2048,128]{1,0:T(8,128)(2,1)S(1)}, bf16[2048,128]{1,0:T(8,128)(2,1)}, u32[]{:S(2)}) %copy-start) | copy-done | bytes 524312
  1.0 0.0 copy-start.1
  1.0 1.0 %copy-done.1 = bf16[2048,128]{1,0:T(8,128)(2,1)S(1)} copy-done((bf16[2048,128]{1,0:T(8,128)(2,1)S(1)}, bf16[2048,128]{1,0:T(8,128)(2,1)}, u32[]{:S(2)}) %copy-start.1) | copy-done | bytes 524312
  2.1 36.6 %shard_map.55 = bf16[1024,1024]{1,0:T(8,128)(2,1)S(1)} custom-call(bf16[1024,2048]{1,0:T(8,128)(2,1)} %tok_hbm.1, bf16[2048,128]{1,0:T(8,128)(2,1)S(1)} %copy-done, bf16[2048,128]{1,0:T(8,128)(2,1)S(1)} %copy-done.1, bf16[2048,1024]{1,0:T(8,128)(2,1)} %wv_hbm.1, bf16[2048,2048]{1,0:T(8,128)(2,1)} %wo_hbm.1), custom_call_target="tpu_custom_call" | custom-call | tf_op jit(solution)/shard_map/pallas_call | solution.py:323
  38.7 1.3 %copy.7 = bf16[1024,1024]{1,0:T(8,128)(2,1)} copy(bf16[1024,1024]{1,0:T(8,128)(2,1)S(1)} %shard_map.55) | data formatting | bytes 4194304
Async XLA Ops:
  0.0 1.0 %copy-start = (bf16[2048,128]{1,0:T(8,128)(2,1)S(1)}, bf16[2048,128]{1,0:T(8,128)(2,1)}, u32[]{:S(2)}) copy-start(bf16[2048,128]{1,0:T(8,128)(2,1)} %wq_hbm.1) | copy-start | bytes 1572868
  1.0 1.0 %copy-start.1 = (bf16[2048,128]{1,0:T(8,128)(2,1)S(1)}, bf16[2048,128]{1,0:T(8,128)(2,1)}, u32[]{:S(2)}) copy-start(bf16[2048,128]{1,0:T(8,128)(2,1)} %wk_hbm.1) | copy-start | bytes 1572868
where the time goes:
time: 40.2 us; the launch traced here: 40 us
  Pallas kernels  36.6 us (91%)
  local copies, waits for them, and re-layouts  3.4 us (8%)
    pallas_call x1, Pallas kernels, per_device(): pl.pallas_call(functools.partial(kernel, n_seq, chunk), out_shape=jax.Sha...  36.6 us
    unnamed x5, local copies, waits for them, and re-layouts  3.4 us

commit v1 on v0

v1 whole, which is shorter than its diff:
```python
import functools

import jax
import jax.numpy as jnp
from jax import lax
from jax.experimental import pallas as pl
from jax.experimental.pallas import tpu as pltpu
from jax.sharding import PartitionSpec as P

KEY_DIM = 16
VALUE_DIM = 128
ROWS = 160
PAIR = 2
LOADS = 2
PLANE = 4
VMEM_LIMIT = 50 * 1024 * 1024
PIECE = PAIR * ROWS // PLANE
MESH = pl.DeviceIdType.MESH
F32 = jnp.float32
BF16 = jnp.bfloat16


def features(u, tail_one, square):
    n = u.shape[1]
    twice = jnp.concatenate([u, u], axis=0)
    parts = [u, u * u * square]
    for d in range(1, KEY_DIM // 2):
        parts.append(u * twice[d : d + KEY_DIM])
    half = KEY_DIM // 2
    parts.append(u[:half] * u[half:])
    row = lax.broadcasted_iota(jnp.int32, (8, n), 0)
    parts.append(jnp.where(row == 0, tail_one, 0.0))
    return jnp.concatenate(parts, axis=0)


def pack_norm(total):
    state, norm = total[:, :VALUE_DIM], total[:, VALUE_DIM:]
    top = norm[:VALUE_DIM]
    rest = norm[VALUE_DIM:]

    def diagonal(block):
        r = lax.broadcasted_iota(jnp.int32, block.shape, 0)
        l = lax.broadcasted_iota(jnp.int32, block.shape, 1)
        return jnp.sum(jnp.where(r == l, block, 0.0), axis=0, keepdims=True)

    first, second = diagonal(top), diagonal(rest)
    r = lax.broadcasted_iota(jnp.int32, (8, VALUE_DIM), 0)
    tail = jnp.where(r == 0, state[ROWS - 8 :], jnp.where(r == 1, first, jnp.where(r == 2, second, 0.0)))
    return jnp.concatenate([state[: ROWS - 8], tail], axis=0)


def unpack_norm(packed):
    tail = packed[ROWS - 8 :]

    def column(row, height):
        r = lax.broadcasted_iota(jnp.int32, (height, VALUE_DIM), 0)
        l = lax.broadcasted_iota(jnp.int32, (height, VALUE_DIM), 1)
        return jnp.sum(jnp.where(r == l, row, 0.0), axis=1, keepdims=True)

    return jnp.concatenate([column(tail[1:2], VALUE_DIM), column(tail[2:3], ROWS - VALUE_DIM)], axis=0)


def kernel(
    n_seq, chunk,
    tok_hbm, wq_hbm, wk_hbm, wv_hbm, wo_hbm, out_ref,
    tok, wqk, wv, wo, vals, qs, qt, kt, kfeat, local, inner, qfeat,
    send_s, recv_s, send_z, recv_z, send_b, recv_b,
    acc, load_sem, tok_sem, v_sem, o_sem, s_ss, s_rs, z_ss, z_rs, b_ss, b_rs, a_ss, a_rs, free_sem,
):
    att = tok
    blocks, rows, block = tok.shape
    heads = vals.shape[0]
    groups = heads // PAIR
    chunks = rows // chunk
    out_blocks = wo.shape[0]
    cols_here = out_blocks * block
    planes = n_seq // PLANE
    seq = lax.axis_index("seq")
    core = lax.axis_index("head")
    p = lax.rem(seq, PLANE)
    z = seq // PLANE
    first = z * PLANE
    peers = [lax.rem(p + o, PLANE) for o in range(1, PLANE)]

    part_rows = rows // LOADS
    load_w = [
        pltpu.make_async_copy(wk_hbm, wqk.at[:, pl.ds(128, 128)], load_sem.at[1]),
        pltpu.make_async_copy(wq_hbm, wqk.at[:, pl.ds(0, 128)], load_sem.at[0]),
    ]
    load_t = [
        [
            pltpu.make_async_copy(
                tok_hbm.at[pl.ds(i * part_rows, part_rows), pl.ds(b * block, block)],
                tok.at[b, pl.ds(i * part_rows, part_rows)], tok_sem.at[i, b])
            for b in range(blocks)
        ]
        for i in range(LOADS)
    ]
    load_o = [
        pltpu.make_async_copy(
            wo_hbm.at[:, pl.ds(pl.multiple_of(core * cols_here + b * block, 128), block)], wo.at[b], o_sem.at[b])
        for b in range(out_blocks)
    ]
    step = PAIR * VALUE_DIM

    def load_v(g):
        return pltpu.make_async_copy(wv_hbm.at[:, pl.ds(g * step, step)], wv.at[g], v_sem.at[g])

    for c in load_w:
        c.start()
    for i in range(LOADS):
        for c in load_t[i]:
            c.start(priority=min(i, 1))

    barrier = pltpu.get_barrier_semaphore()
    for q in peers:
        pl.semaphore_signal(barrier, inc=1, device_id=(first + q, core), device_id_type=MESH)
    for o in range(1, planes):
        there = lax.rem(z + o, planes) * PLANE + p
        pl.semaphore_signal(barrier, inc=1, device_id=(there, core), device_id_type=MESH)
    pl.semaphore_signal(barrier, inc=1, device_id=(seq, 1 - core), device_id_type=MESH)
    greetings = PLANE - 1 + planes - 1 + 1

    def copy_s(g, q, slot):
        return pltpu.make_async_remote_copy(
            src_ref=send_s.at[g, q], dst_ref=recv_s.at[g, slot], send_sem=s_ss.at[g, q], recv_sem=s_rs.at[g, slot],
            device_id=(first + q, core), device_id_type=MESH)

    def copy_z(g, there, slot):
        return pltpu.make_async_remote_copy(
            src_ref=send_z.at[g], dst_ref=recv_z.at[g, slot], send_sem=z_ss.at[g, there], recv_sem=z_rs.at[g, slot],
            device_id=(there * PLANE + p, core), device_id_type=MESH)

    def copy_b(g, q, slot):
        return pltpu.make_async_remote_copy(
            src_ref=send_b.at[g, q], dst_ref=recv_b.at[g, slot], send_sem=b_ss.at[g, q], recv_sem=b_rs.at[g, slot],
            device_id=(first + q, core), device_id_type=MESH)

    own_at, peer_at = core * groups, (1 - core) * groups

    def copy_a(g, base):
        return pltpu.make_async_remote_copy(
            src_ref=att.at[base + g], dst_ref=att.at[base + g], send_sem=a_ss.at[g], recv_sem=a_rs.at[g],
            device_id=(seq, 1 - core), device_id_type=MESH)

    def gather_pieces(g):
        for q in peers:
            copy_s(g, q, p).start()

    def send_up(g):
        for q in peers:
            copy_s(g, q, q).wait_recv()
        total = recv_s[g, 0].astype(F32)
        for q in range(1, PLANE):
            total = total + recv_s[g, q].astype(F32)
        send_z[g] = total.astype(BF16)

        def send(i, _):
            copy_z(g, planes - 1 - i, z).start()
            return 0

        lax.fori_loop(0, planes - 1 - z, send, 0)

    def give_back(g):
        def take(i, total):
            copy_z(g, i, i).wait_recv()
            return total + recv_z[g, i].astype(F32)

        total = lax.fori_loop(0, z, take, jnp.zeros((PIECE, VALUE_DIM), F32))
        for q in range(PLANE):
            send_b[g, q] = total.astype(BF16)
            total = total + recv_s[g, q].astype(F32)
        for q in peers:
            copy_b(g, q, p).start()
        recv_b[g, p] = send_b[g, p]

    def token_rows(begin, end):
        return jnp.concatenate([tok[b, pl.ds(begin, end - begin)] for b in range(blocks)], axis=1)

    for c in load_w:
        c.wait()
    for i in range(LOADS):
        for c in load_t[i]:
            c.wait()
        if i == 0:
            for g in range(groups):
                load_v(g).start(priority=1)
        part = pl.ds(i * part_rows, part_rows)
        qk = jnp.dot(token_rows(i * part_rows, (i + 1) * part_rows), wqk[...], preferred_element_type=F32)
        qk = qk.astype(BF16).astype(F32)
        q = qk[:, :128] * 0.25
        qs[part] = q.astype(BF16)
        for c in range(part_rows // chunk):
            at = i * (part_rows // chunk) + c
            qt[at] = q[c * chunk : (c + 1) * chunk].T
            kt[at] = qk[c * chunk : (c + 1) * chunk, 128:].T
    for c in load_o:
        c.start(priority=1)

    def head_rows(h):
        if isinstance(h, int):
            return pl.ds(h * KEY_DIM, KEY_DIM)
        return pl.ds(pl.multiple_of(h * KEY_DIM, KEY_DIM), KEY_DIM)

    def key_features(g):
        for i in range(PAIR):
            h = g * PAIR + i
            for c in range(chunks):
                kfeat[h % (2 * PAIR), c] = features(kt[c, head_rows(h)], 1.0, 1.0).astype(BF16)

    def values(g, begin, end):
        part = pl.ds(begin, end - begin)
        v = jnp.dot(token_rows(begin, end), wv[g], preferred_element_type=F32).astype(BF16)
        for i in range(PAIR):
            vals[g * PAIR + i, part] = v[:, i * VALUE_DIM : (i + 1) * VALUE_DIM]

    def states(g):
        ones = jnp.ones((chunk, VALUE_DIM), BF16)
        for i in range(PAIR):
            h = g * PAIR + i
            total = jnp.zeros((ROWS, 2 * VALUE_DIM), F32)
            for c in range(chunks):
                span = pl.ds(c * chunk, chunk)
                local[h, c] = total
                wide = jnp.concatenate([vals[h, span], ones], axis=1)
                total = total + jnp.dot(kfeat[h % (2 * PAIR), c], wide, preferred_element_type=F32)
            packed = pack_norm(total).astype(BF16)
            send_s[g, 2 * i] = packed[:PIECE]
            send_s[g, 2 * i + 1] = packed[PIECE:]
        recv_s[g, p] = send_s[g, p]

    for g in range(groups):
        load_v(g).wait()
        values(g, 0, rows // 2)
        key_features(g)
        if g > 0:
            states(g - 1)
        values(g, rows // 2, rows)
        if g > 0:
            if g == 1:
                pl.semaphore_wait(barrier, greetings)
            gather_pieces(g - 1)
    pl.semaphore_signal(free_sem, inc=1, device_id=(seq, 1 - core), device_id_type=MESH)
    states(groups - 1)
    gather_pieces(groups - 1)

    def inner_head(h):
        row_head = lax.broadcasted_iota(jnp.int32, (128, chunk), 0) // KEY_DIM
        r = lax.broadcasted_iota(jnp.int32, (chunk, chunk), 0)
        l = lax.broadcasted_iota(jnp.int32, (chunk, chunk), 1)
        ones = jnp.ones((chunk, VALUE_DIM), BF16)
        for c in range(chunks):
            span = pl.ds(c * chunk, chunk)
            k_own = jnp.where(row_head == h, kt[c], 0.0).astype(BF16)
            s = jnp.dot(qs[span], k_own, preferred_element_type=F32)
            s1 = s + 1.0
            taylor = jnp.where(l <= r, 0.5 * (s1 * s1) + 0.5, 0.0).astype(BF16)
            wide = jnp.concatenate([vals[h, span], ones], axis=1)
            inner[h, span] = jnp.dot(taylor, wide, preferred_element_type=F32)
            feat = features(qt[c, head_rows(h)], 1.0, 0.5)
            qfeat[h, span] = feat.T.astype(BF16)

    def inner_step(g, _):
        for i in range(PAIR):
            inner_head(g * PAIR + i)
        send_up(g)
        return 0

    lax.fori_loop(0, groups, inner_step, 0)

    def back_step(g, _):
        give_back(g)
        return 0

    lax.fori_loop(0, groups, back_step, 0)

    def outer(g):
        for q in peers:
            copy_b(g, q, q).wait_recv()
        for i in range(PAIR):
            h = g * PAIR + i
            packed = jnp.concatenate([recv_b[g, 2 * i], recv_b[g, 2 * i + 1]], axis=0).astype(F32)
            norm = jnp.broadcast_to(unpack_norm(packed), (ROWS, VALUE_DIM))
            entering = jnp.concatenate([packed, norm], axis=1)
            for c in range(chunks):
                span = pl.ds(c * chunk, chunk)
                prefix = (entering + local[h, c]).astype(BF16)
                total = inner[h, span] + jnp.dot(qfeat[h, span], prefix, preferred_element_type=F32)
                result = total[:, :VALUE_DIM] / total[:, VALUE_DIM:]
                att[own_at + g, span, pl.ds(i * VALUE_DIM, VALUE_DIM)] = result.astype(BF16)
        copy_a(g, own_at).start()

    def project(g, begin, end):
        copy_a(g, peer_at).wait_recv()
        here = pl.ds(pl.multiple_of((own_at + g) * step, step), step)
        there = pl.ds(pl.multiple_of((peer_at + g) * step, step), step)
        both = jnp.concatenate([att[own_at + g], att[peer_at + g]], axis=1)
        for b in range(out_blocks):
            w = jnp.concatenate([wo[b, here], wo[b, there]], axis=0)
            part = jnp.dot(both, w, preferred_element_type=F32)
            if not begin:
                part = part + acc[b]
            if end:
                out_ref[:, pl.ds(b * block, block)] = part.astype(BF16)
            else:
                acc[b] = part

    pl.semaphore_wait(free_sem, 1)
    outer(0)
    for c in load_o:
        c.wait()
    for g in range(1, groups):
        outer(g)
        project(g - 1, g == 1, False)
    project(groups - 1, False, True)

    def finish(g, _):
        copy_a(g, own_at).wait_send()
        for q in peers:
            copy_s(g, q, p).wait_send()
            copy_b(g, q, p).wait_send()

        def sent(i, _):
            copy_z(g, planes - 1 - i, z).wait_send()
            return 0

        lax.fori_loop(0, planes - 1 - z, sent, 0)
        return 0

    lax.fori_loop(0, groups, finish, 0)


def per_device(tokens, w_query, w_key, w_value, w_out):
    n_seq = lax.axis_size("seq")
    rows, width = tokens.shape
    heads = w_query.shape[1] // KEY_DIM
    groups = heads // PAIR
    planes = n_seq // PLANE
    chunk = min(256, rows)
    block = PAIR * VALUE_DIM
    cols = w_out.shape[1] // lax.axis_size("head")
    vm = pltpu.VMEM
    dma = pltpu.SemaphoreType.DMA
    return pl.pallas_call(
        functools.partial(kernel, n_seq, chunk),
        out_shape=jax.ShapeDtypeStruct((rows, cols), BF16),
        in_specs=[pl.BlockSpec(memory_space=pltpu.HBM)] * 5,
        out_specs=pl.BlockSpec(memory_space=pltpu.VMEM),
        scratch_shapes=[
            vm((width // block, rows, block), BF16),
            vm((width, 256), BF16),
            vm((groups, width, PAIR * VALUE_DIM), BF16),
            vm((cols // block, w_out.shape[0], block), BF16),
            vm((heads, rows, VALUE_DIM), BF16),
            vm((rows, 128), BF16),
            vm((rows // chunk, 128, chunk), F32),
            vm((rows // chunk, 128, chunk), F32),
            vm((2 * PAIR, rows // chunk, ROWS, chunk), BF16),
            vm((heads, rows // chunk, ROWS, 2 * VALUE_DIM), F32),
            vm((heads, rows, 2 * VALUE_DIM), F32),
            vm((heads, rows, ROWS), BF16),
            vm((groups, PLANE, PIECE, VALUE_DIM), BF16),
            vm((groups, PLANE, PIECE, VALUE_DIM), BF16),
            vm((groups, PIECE, VALUE_DIM), BF16),
            vm((groups, planes, PIECE, VALUE_DIM), BF16),
            vm((groups, PLANE, PIECE, VALUE_DIM), BF16),
            vm((groups, PLANE, PIECE, VALUE_DIM), BF16),
            vm((cols // block, rows, block), F32),
            dma((2,)), dma((LOADS, width // block)), dma((groups,)), dma((cols // block,)),
            dma((groups, PLANE)), dma((groups, PLANE)),
            dma((groups, planes)), dma((groups, planes)),
            dma((groups, PLANE)), dma((groups, PLANE)),
            dma((groups,)), dma((groups,)), pltpu.SemaphoreType.REGULAR,
        ],
        compiler_params=pltpu.CompilerParams(
            collective_id=0, has_side_effects=True, vmem_limit_bytes=VMEM_LIMIT
        ),
    )(*(pltpu.with_memory_space_constraint(a, pltpu.HBM) for a in (tokens, w_query, w_key, w_value, w_out)))


def solution(mesh):
    in_specs = (P("seq", None), P(None, "head"), P(None, "head"), P(None, "head"), P())
    return jax.shard_map(
        per_device, mesh=mesh, in_specs=in_specs, out_specs=P("seq", "head"), check_vma=False
    )
```

time: 40.2 us -> 33.4 us (0.83)
  the two profiles are of different devices: /device:TPU:25 before, /device:TPU:17 now
where the time goes in v1:
time: 33.4 us; the launch traced here: 33.3 us
  Pallas kernels  32 us (96%)
  local copies, waits for them, and re-layouts  1.32 us (4%)
    pallas_call x1, Pallas kernels, per_device(): pl.pallas_call(functools.partial(kernel, n_seq, chunk), out_shape=jax.Sha...  32 us
    unnamed x1, local copies, waits for them, and re-layouts  1.32 us

profile of v1, /device:TPU:17, one launch (start us, length us, event | category | flops | bytes accessed | tf_op | source)
XLA Modules:
  0.0 33.3 jit_solution(3090051661350782510)
XLA Ops:
  0.0 32.0 %shard_map.55 = bf16[1024,1024]{1,0:T(8,128)(2,1)S(1)} custom-call(bf16[1024,2048]{1,0:T(8,128)(2,1)} %tok_hbm.1, bf16[2048,128]{1,0:T(8,128)(2,1)} %wq_hbm.1, bf16[2048,128]{1,0:T(8,128)(2,1)} %wk_hbm.1, bf16[2048,1024]{1,0:T(8,128)(2,1)} %wv_hbm.1, bf16[2048,2048]{1,0:T(8,128)(2,1)} %wo_hbm.1), custom_call_target="tpu_custom_call" | custom-call | tf_op jit(solution)/shard_map/pallas_call | solution.py:344
  32.0 1.3 %copy.7 = bf16[1024,1024]{1,0:T(8,128)(2,1)} copy(bf16[1024,1024]{1,0:T(8,128)(2,1)S(1)} %shard_map.55) | data formatting | bytes 4194304

commit v2 on v1

--- a/solution.py
+++ b/solution.py
@@ -13,7 +13,7 @@
 PAIR = 2
 LOADS = 2
 PLANE = 4
-VMEM_LIMIT = 50 * 1024 * 1024
+VMEM_LIMIT = 51 * 1024 * 1024
 PIECE = PAIR * ROWS // PLANE
 MESH = pl.DeviceIdType.MESH
 F32 = jnp.float32
@@ -63,9 +63,9 @@
 def kernel(
     n_seq, chunk,
     tok_hbm, wq_hbm, wk_hbm, wv_hbm, wo_hbm, out_ref,
-    tok, wqk, wv, wo, vals, qs, qt, kt, kfeat, local, inner, qfeat,
+    tok, wqkv, wo, vals, qs, qt, kt, kfeat, local, inner, qfeat,
     send_s, recv_s, send_z, recv_z, send_b, recv_b,
-    acc, load_sem, tok_sem, v_sem, o_sem, s_ss, s_rs, z_ss, z_rs, b_ss, b_rs, a_ss, a_rs, free_sem,
+    acc, w_sem, tok_sem, o_sem, s_ss, s_rs, z_ss, z_rs, b_ss, b_rs, a_ss, a_rs, free_sem,
 ):
     att = tok
     blocks, rows, block = tok.shape
@@ -80,13 +80,22 @@
     p = lax.rem(seq, PLANE)
     z = seq // PLANE
     first = z * PLANE
-    peers = [lax.rem(p + o, PLANE) for o in range(1, PLANE)]
+    peers = [PLANE - 1 - p, p + 1 - 2 * lax.rem(p, 2), lax.rem(p + 2, PLANE)]
 
     part_rows = rows // LOADS
-    load_w = [
-        pltpu.make_async_copy(wk_hbm, wqk.at[:, pl.ds(128, 128)], load_sem.at[1]),
-        pltpu.make_async_copy(wq_hbm, wqk.at[:, pl.ds(0, 128)], load_sem.at[0]),
-    ]
+    left, right = pl.ds(0, VALUE_DIM), pl.ds(VALUE_DIM, VALUE_DIM)
+    load_w = [[
+        pltpu.make_async_copy(wk_hbm, wqkv.at[0, :, left], w_sem.at[0, 0]),
+        pltpu.make_async_copy(wv_hbm.at[:, left], wqkv.at[0, :, right], w_sem.at[0, 1]),
+    ]]
+    for x in range(1, groups):
+        at = pl.ds((2 * x - 1) * VALUE_DIM, block)
+        load_w.append([pltpu.make_async_copy(wv_hbm.at[:, at], wqkv.at[x], w_sem.at[x, 0])])
+    at = pl.ds((heads - 1) * VALUE_DIM, VALUE_DIM)
+    load_w.append([
+        pltpu.make_async_copy(wv_hbm.at[:, at], wqkv.at[groups, :, left], w_sem.at[groups, 0]),
+        pltpu.make_async_copy(wq_hbm, wqkv.at[groups, :, right], w_sem.at[groups, 1]),
+    ])
     load_t = [
         [
             pltpu.make_async_copy(
@@ -103,14 +112,14 @@
     ]
     step = PAIR * VALUE_DIM
 
-    def load_v(g):
-        return pltpu.make_async_copy(wv_hbm.at[:, pl.ds(g * step, step)], wv.at[g], v_sem.at[g])
-
-    for c in load_w:
+    for c in load_w[0]:
         c.start()
     for i in range(LOADS):
         for c in load_t[i]:
-            c.start(priority=min(i, 1))
+            c.start()
+    for x in range(1, groups + 1):
+        for c in load_w[x]:
+            c.start(priority=1)
 
     barrier = pltpu.get_barrier_semaphore()
     for q in peers:
@@ -144,6 +153,7 @@
             device_id=(seq, 1 - core), device_id_type=MESH)
 
     def gather_pieces(g):
+        recv_s[g, p] = send_s[g, p]
         for q in peers:
             copy_s(g, q, p).start()
 
@@ -156,10 +166,10 @@
         send_z[g] = total.astype(BF16)
 
         def send(i, _):
-            copy_z(g, planes - 1 - i, z).start()
+            copy_z(g, i if g % 2 else planes + z - i, z).start()
             return 0
 
-        lax.fori_loop(0, planes - 1 - z, send, 0)
+        lax.fori_loop(z + 1, planes, send, 0)
 
     def give_back(g):
         def take(i, total):
@@ -177,71 +187,79 @@
     def token_rows(begin, end):
         return jnp.concatenate([tok[b, pl.ds(begin, end - begin)] for b in range(blocks)], axis=1)
 
-    for c in load_w:
+    def head_rows(h):
+        if isinstance(h, int):
+            return pl.ds(h * KEY_DIM, KEY_DIM)
+        return pl.ds(pl.multiple_of(h * KEY_DIM, KEY_DIM), KEY_DIM)
+
+    def transposed(ref, part, begin):
+        for c in range(part.shape[0] // chunk):
+            ref[begin // chunk + c] = part[c * chunk : (c + 1) * chunk].T
+
+    def project_in(x, begin, end):
+        part = pl.ds(begin, end - begin)
+        tokens = jnp.concatenate([tok[b, part] for b in range(blocks)], axis=1)
+        both = jnp.dot(tokens, wqkv[x], preferred_element_type=F32).astype(BF16)
+        lo, hi = both[:, :VALUE_DIM], both[:, VALUE_DIM:]
+        if x == 0:
+            transposed(kt, lo.astype(F32), begin)
+            vals[0, part] = hi
+            return
+        vals[2 * x - 1, part] = lo
+        if x < groups:
+            vals[2 * x, part] = hi
+            return
+        q = hi.astype(F32) * 0.25
+        qs[part] = q.astype(BF16)
+        transposed(qt, q, begin)
+
+    def key_features(h):
+        for c in range(chunks):
+            kfeat[h, c] = features(kt[c, head_rows(h)], 1.0, 1.0).astype(BF16)
+
+    def state(h):
+        ones = jnp.ones((chunk, VALUE_DIM), BF16)
+        total = jnp.zeros((ROWS, 2 * VALUE_DIM), F32)
+        for c in range(chunks):
+            span = pl.ds(c * chunk, chunk)
+            local[h, c] = total
+            wide = jnp.concatenate([vals[h, span], ones], axis=1)
+            total = total + jnp.dot(kfeat[h, c], wide, preferred_element_type=F32)
+        packed = pack_norm(total).astype(BF16)
+        g, i = h // PAIR, h % PAIR
+        send_s[g, 2 * i] = packed[:PIECE]
+        send_s[g, 2 * i + 1] = packed[PIECE:]
+
+    for c in load_w[0]:
         c.wait()
     for i in range(LOADS):
         for c in load_t[i]:
             c.wait()
-        if i == 0:
-            for g in range(groups):
-                load_v(g).start(priority=1)
-        part = pl.ds(i * part_rows, part_rows)
-        qk = jnp.dot(token_rows(i * part_rows, (i + 1) * part_rows), wqk[...], preferred_element_type=F32)
-        qk = qk.astype(BF16).astype(F32)
-        q = qk[:, :128] * 0.25
-        qs[part] = q.astype(BF16)
-        for c in range(part_rows // chunk):
-            at = i * (part_rows // chunk) + c
-            qt[at] = q[c * chunk : (c + 1) * chunk].T
-            kt[at] = qk[c * chunk : (c + 1) * chunk, 128:].T
+        project_in(0, i * part_rows, (i + 1) * part_rows)
     for c in load_o:
         c.start(priority=1)
 
-    def head_rows(h):
-        if isinstance(h, int):
-            return pl.ds(h * KEY_DIM, KEY_DIM)
-        return pl.ds(pl.multiple_of(h * KEY_DIM, KEY_DIM), KEY_DIM)
-
-    def key_features(g):
-        for i in range(PAIR):
-            h = g * PAIR + i
-            for c in range(chunks):
-                kfeat[h % (2 * PAIR), c] = features(kt[c, head_rows(h)], 1.0, 1.0).astype(BF16)
-
-    def values(g, begin, end):
-        part = pl.ds(begin, end - begin)
-        v = jnp.dot(token_rows(begin, end), wv[g], preferred_element_type=F32).astype(BF16)
-        for i in range(PAIR):
-            vals[g * PAIR + i, part] = v[:, i * VALUE_DIM : (i + 1) * VALUE_DIM]
-
-    def states(g):
-        ones = jnp.ones((chunk, VALUE_DIM), BF16)
-        for i in range(PAIR):
-            h = g * PAIR + i
-            total = jnp.zeros((ROWS, 2 * VALUE_DIM), F32)
-            for c in range(chunks):
-                span = pl.ds(c * chunk, chunk)
-                local[h, c] = total
-                wide = jnp.concatenate([vals[h, span], ones], axis=1)
-                total = total + jnp.dot(kfeat[h % (2 * PAIR), c], wide, preferred_element_type=F32)
-            packed = pack_norm(total).astype(BF16)
-            send_s[g, 2 * i] = packed[:PIECE]
-            send_s[g, 2 * i + 1] = packed[PIECE:]
-        recv_s[g, p] = send_s[g, p]
-
-    for g in range(groups):
-        load_v(g).wait()
-        values(g, 0, rows // 2)
-        key_features(g)
-        if g > 0:
-            states(g - 1)
-        values(g, rows // 2, rows)
-        if g > 0:
-            if g == 1:
-                pl.semaphore_wait(barrier, greetings)
-            gather_pieces(g - 1)
+    for x in range(1, groups + 1):
+        for c in load_w[x]:
+            c.wait()
+        if x == 1:
+            key_features(0)
+        key_features(2 * x - 1)
+        project_in(x, 0, rows // 2)
+        if x > 2:
+            state(2 * x - 3)
+        state(2 * x - 2)
+        if x < groups:
+            key_features(2 * x)
+        project_in(x, rows // 2, rows)
+        if x == 1:
+            pl.semaphore_wait(barrier, greetings)
+            state(1)
+            gather_pieces(0)
+        if x > 2:
+            gather_pieces(x - 2)
     pl.semaphore_signal(free_sem, inc=1, device_id=(seq, 1 - core), device_id_type=MESH)
-    states(groups - 1)
+    state(heads - 1)
     gather_pieces(groups - 1)
 
     def inner_head(h):
@@ -260,20 +278,6 @@
             feat = features(qt[c, head_rows(h)], 1.0, 0.5)
             qfeat[h, span] = feat.T.astype(BF16)
 
-    def inner_step(g, _):
-        for i in range(PAIR):
-            inner_head(g * PAIR + i)
-        send_up(g)
-        return 0
-
-    lax.fori_loop(0, groups, inner_step, 0)
-
-    def back_step(g, _):
-        give_back(g)
-        return 0
-
-    lax.fori_loop(0, groups, back_step, 0)
-
     def outer(g):
         for q in peers:
             copy_b(g, q, q).wait_recv()
@@ -290,13 +294,14 @@
                 att[own_at + g, span, pl.ds(i * VALUE_DIM, VALUE_DIM)] = result.astype(BF16)
         copy_a(g, own_at).start()
 
-    def project(g, begin, end):
-        copy_a(g, peer_at).wait_recv()
-        here = pl.ds(pl.multiple_of((own_at + g) * step, step), step)
-        there = pl.ds(pl.multiple_of((peer_at + g) * step, step), step)
-        both = jnp.concatenate([att[own_at + g], att[peer_at + g]], axis=1)
+    def project(g, own, peer, begin, end):
+        bases = ([own_at] if own else []) + ([peer_at] if peer else [])
+        if peer:
+            copy_a(g, peer_at).wait_recv()
+        rows_of = [pl.ds(pl.multiple_of((base + g) * step, step), step) for base in bases]
+        both = jnp.concatenate([att[base + g] for base in bases], axis=1)
         for b in range(out_blocks):
-            w = jnp.concatenate([wo[b, here], wo[b, there]], axis=0)
+            w = jnp.concatenate([wo[b, r] for r in rows_of], axis=0)
             part = jnp.dot(both, w, preferred_element_type=F32)
             if not begin:
                 part = part + acc[b]
@@ -305,14 +310,31 @@
             else:
                 acc[b] = part
 
+    def inner_pair(g):
+        for i in range(PAIR):
+            inner_head(g * PAIR + i)
+
+    last = groups - 1
+    send_up(0)
+    inner_pair(0)
+    for g in range(1, last):
+        inner_pair(g)
+        send_up(g)
+    send_up(last)
+    give_back(0)
+    inner_pair(last)
+    for g in range(1, last):
+        give_back(g)
     pl.semaphore_wait(free_sem, 1)
     outer(0)
+    give_back(last)
     for c in load_o:
         c.wait()
     for g in range(1, groups):
         outer(g)
-        project(g - 1, g == 1, False)
-    project(groups - 1, False, True)
+        project(g - 1, True, True, g == 1, False)
+    project(last, True, False, False, False)
+    project(last, False, True, False, True)
 
     def finish(g, _):
         copy_a(g, own_at).wait_send()
@@ -348,14 +370,13 @@
         out_specs=pl.BlockSpec(memory_space=pltpu.VMEM),
         scratch_shapes=[
             vm((width // block, rows, block), BF16),
-            vm((width, 256), BF16),
-            vm((groups, width, PAIR * VALUE_DIM), BF16),
+            vm((groups + 1, width, block), BF16),
             vm((cols // block, w_out.shape[0], block), BF16),
             vm((heads, rows, VALUE_DIM), BF16),
             vm((rows, 128), BF16),
             vm((rows // chunk, 128, chunk), F32),
             vm((rows // chunk, 128, chunk), F32),
-            vm((2 * PAIR, rows // chunk, ROWS, chunk), BF16),
+            vm((heads, rows // chunk, ROWS, chunk), BF16),
             vm((heads, rows // chunk, ROWS, 2 * VALUE_DIM), F32),
             vm((heads, rows, 2 * VALUE_DIM), F32),
             vm((heads, rows, ROWS), BF16),
@@ -366,7 +387,7 @@
             vm((groups, PLANE, PIECE, VALUE_DIM), BF16),
             vm((groups, PLANE, PIECE, VALUE_DIM), BF16),
             vm((cols // block, rows, block), F32),
-            dma((2,)), dma((LOADS, width // block)), dma((groups,)), dma((cols // block,)),
+            dma((groups + 1, 2)), dma((LOADS, width // block)), dma((cols // block,)),
             dma((groups, PLANE)), dma((groups, PLANE)),
             dma((groups, planes)), dma((groups, planes)),
             dma((groups, PLANE)), dma((groups, PLANE)),

time: 33.4 us -> 32.8 us (0.982)
  the two profiles are of different devices: /device:TPU:17 before, /device:TPU:25 now
where the time goes in v2:
time: 32.8 us; the launch traced here: 32.6 us
  Pallas kernels  31.3 us (95%)
  local copies, waits for them, and re-layouts  1.32 us (4%)
    pallas_call x1, Pallas kernels, per_device(): pl.pallas_call(functools.partial(kernel, n_seq, chunk), out_shape=jax.Sha...  31.3 us
    unnamed x1, local copies, waits for them, and re-layouts  1.32 us

profile of v2, /device:TPU:25, one launch (start us, length us, event | category | flops | bytes accessed | tf_op | source)
XLA Modules:
  0.0 32.6 jit_solution(17499530281835869526)
XLA Ops:
  0.0 31.3 %shard_map.55 = bf16[1024,1024]{1,0:T(8,128)(2,1)S(1)} custom-call(bf16[1024,2048]{1,0:T(8,128)(2,1)} %tok_hbm.1, bf16[2048,128]{1,0:T(8,128)(2,1)} %wq_hbm.1, bf16[2048,128]{1,0:T(8,128)(2,1)} %wk_hbm.1, bf16[2048,1024]{1,0:T(8,128)(2,1)} %wv_hbm.1, bf16[2048,2048]{1,0:T(8,128)(2,1)} %wo_hbm.1), custom_call_target="tpu_custom_call" | custom-call | tf_op jit(solution)/shard_map/pallas_call | solution.py:366
  31.3 1.3 %copy.7 = bf16[1024,1024]{1,0:T(8,128)(2,1)} copy(bf16[1024,1024]{1,0:T(8,128)(2,1)S(1)} %shard_map.55) | data formatting | bytes 4194304
